TPU v7x, 32 devices: a whole 2x2x4 slice. The times are simulated.
32 devices in a mesh: clip: 2 (over y), ha: 8 (over z, x), ta: 2 (over core).
Axes of the slice: x: 2, y: 2, z: 4, core: 2. Of those that a mesh axis runs over, the one named last changes fastest.
Arguments:
- latent_tokens: bfloat16 [16, 512, 64], P('clip', ('ha', 'ta')), parts along dimension 0, may hold values from -8 to 8
- w_in: bfloat16 [3, 3, 3, 16, 384], replicated, may hold values from -0.3125 to 0.3125
- b_in: float32 [384], replicated, may hold values from -3 to 3
- gn_gain: float32 [384], replicated, may hold values from 0.1 to 1.9
- gn_shift: float32 [384], replicated, may hold values from -3 to 3
- w_mid: bfloat16 [3, 3, 3, 384, 384], replicated, may hold values from -0.109375 to 0.109375
- b_mid: float32 [384], replicated, may hold values from -3 to 3
Outputs:
- decoded: bfloat16 [16, 16, 128, 384], P(('clip', 'ta'), 'ha'), parts along dimension 0
There are 2 independent parts, one for each index of `clip`. A program takes and returns all parts, laid end to end along the dimension named above; an argument that names none is the same for every part. Nothing has to cross between parts.
All inputs are finite; a program needn't handle non-finite values.
Results may differ from a plain program's by a relative error of at most 0.0054.
Values may be sent and summed in bfloat16 or wider, within the bound.
A program may use at most 64 MiB of HBM per device.

v0:
```python
import jax
import jax.numpy as jnp
from jax import lax
from jax.sharding import PartitionSpec as P

GROUPS = 32
H_DEV = 2
W = 128
eps = 1e-06


def passed_along(value, axis, by):
    devices = lax.axis_size(axis)
    pairs = [(i, i + by) for i in range(devices) if 0 <= i + by < devices]
    return lax.ppermute(value, axis, pairs)


def extended_2(value, sides, width):
    for axis, dim in sides:
        devices, length = (lax.axis_size(axis), value.shape[dim])
        up = [(i, (i + 1) % devices) for i in range(devices - 1)]
        down = [(j, i) for i, j in up]
        last = lax.slice_in_dim(value, length - width, length, axis=dim)
        first = lax.slice_in_dim(value, 0, width, axis=dim)
        before = lax.ppermute(last, axis, up)
        after = lax.ppermute(first, axis, down)
        value = jnp.concatenate([before, value, after], axis=dim)
    return value


def unpatch(tokens, rows, cols):
    frames = tokens.shape[0]
    latent_ch = tokens.shape[2] // 4
    blocks = tokens.reshape(frames, rows // 2, cols // 2, 2, 2, latent_ch)
    return blocks.transpose(0, 1, 3, 2, 4, 5).reshape(frames, rows, cols, latent_ch)


def pad_cols(field):
    return jnp.pad(field, ((0, 0), (0, 0), (1, 1), (0, 0)))


def input_conv(padded, w_in, b_in, frames, rows, cols):
    pieces = [
        padded[frame_tap : frame_tap + frames, row_tap : row_tap + rows, col_tap : col_tap + cols]
        for frame_tap in range(3)
        for row_tap in range(3)
        for col_tap in range(3)
    ]
    stacked = jnp.concatenate(pieces, axis=-1).reshape(frames * rows * cols, -1)
    result = jnp.dot(
        stacked, w_in.reshape(stacked.shape[1], -1), preferred_element_type=jnp.float32
    )
    return (result + b_in).reshape(frames, rows, cols, -1)


def middle_conv(padded, w_mid, frames, rows, cols):
    channels = padded.shape[-1]
    total = jnp.zeros((frames * rows * cols, w_mid.shape[-1]), jnp.float32)
    for frame_tap in range(3):
        for row_tap in range(3):
            slab = jnp.concatenate(
                [
                    padded[
                        frame_tap : frame_tap + frames,
                        row_tap : row_tap + rows,
                        col_tap : col_tap + cols,
                    ]
                    for col_tap in range(3)
                ],
                axis=-1,
            ).reshape(frames * rows * cols, 3 * channels)
            total = total + jnp.dot(
                slab,
                w_mid[frame_tap, row_tap].reshape(3 * channels, -1),
                preferred_element_type=jnp.float32,
            )
    return total.reshape(frames, rows, cols, -1)


def group_totals(field):
    grouped = field.reshape(-1, GROUPS, field.shape[-1] // GROUPS)
    return jnp.sum(grouped, axis=(0, 2))


def normalize(hidden, mean, var, gn_gain, gn_shift):
    members = hidden.shape[-1] // GROUPS
    mean_chan = jnp.repeat(mean, members)
    scale_chan = jnp.repeat(lax.rsqrt(var + eps), members)
    scaled = (hidden.astype(jnp.float32) - mean_chan) * scale_chan * gn_gain + gn_shift
    return jax.nn.silu(scaled).astype(jnp.bfloat16)


def body(latent_tokens, w_in, b_in, gn_gain, gn_shift, w_mid, b_mid):
    rows = H_DEV
    cols = W
    moved = lax.all_to_all(latent_tokens, "ta", split_axis=0, concat_axis=1, tiled=True)
    latent = unpatch(moved, rows, cols)
    frames = latent.shape[0]
    earlier = passed_along(latent, "ta", 1)
    extended = jnp.concatenate([earlier, latent], axis=0)
    framed = extended_2(extended, (("ha", 1),), 2)
    wide_hidden = input_conv(pad_cols(framed), w_in, b_in, frames + 2, rows + 2, cols).astype(
        jnp.bfloat16
    )
    hidden = wide_hidden[2:, 1 : rows + 1]
    values = lax.optimization_barrier(hidden).astype(jnp.float32)
    members = values.shape[-1] // GROUPS
    count = float(lax.axis_size("ha") * lax.axis_size("ta") * frames * rows * cols * members)
    mean = lax.psum(group_totals(values), ("ha", "ta")) / count
    centered = values - jnp.repeat(mean, members)
    var = lax.psum(group_totals(centered * centered), ("ha", "ta")) / count
    active = normalize(wide_hidden, mean, var, gn_gain, gn_shift)
    frame_pos = lax.axis_index("ta") * frames + jnp.arange(frames + 2, dtype=jnp.int32) - 2
    row_pos = lax.axis_index("ha") * rows + jnp.arange(rows + 2, dtype=jnp.int32) - 1
    inside = (
        (frame_pos >= 0)[:, None]
        & (row_pos >= 0)[None, :]
        & (row_pos < rows * lax.axis_size("ha"))[None, :]
    )
    padded = jnp.where(inside[:, :, None, None], active, jnp.zeros_like(active))
    branch = middle_conv(pad_cols(padded), w_mid, frames, rows, cols)
    return (values + branch + b_mid).astype(jnp.bfloat16)


def solution(mesh):
    placed = (P("clip", ("ha", "ta"), None), P(), P(), P(), P(), P(), P())
    return jax.shard_map(
        body,
        mesh=mesh,
        in_specs=placed,
        out_specs=P(("clip", "ta"), "ha", None, None),
        check_vma=False,
    )
```

profile of v0, /device:TPU:0, one launch (start us, length us, event | category | flops | bytes accessed | tf_op | source)
XLA Modules:
  0.0 131.4 jit_solution(58256040233946923)
XLA Ops:
  0.0 1.0 reshape.124
  1.0 3.7 %all_to_all.15 = bf16[2,2,4096]{2,1,0:T(2,128)(2,1)S(1)} all-to-all(bf16[2,2,4096]{2,1,0:T(2,128)(2,1)S(1)} %reshape.124), channel_id=1, replica_groups=mesh['clip'=2,'ha'=8,'ta'=2] {'ta'}, dimensions={0} | all-to-all | bytes 65536 | tf_op jit(solution)/shard_map/all_to_all | solution.py:96
  5.1 0.2 copy.15
  5.3 2.1 %collective-permute-start = (bf16[4,2,128,16]{3,2,1,0:T(8,128)(2,1)S(1)}, bf16[4,2,128,16]{3,2,1,0:T(8,128)(2,1)S(1)}, u32[]{:S(2)}, u32[]{:S(2)}) collective-permute-start(bf16[4,2,128,16]{3,2,1,0:T(8,128)(2,1)S(1)} %bitcast.63), channel_id=1, source_target_pairs={{0,1},{2,3},{4,5},{6,7},{8,9},{10,11},{12,13},{14,15},{16,17},{18,... | collective-permute-start | bytes 98312 | tf_op jit(solution)/shard_map/ppermute | solution.py:15
  7.4 5.7 %fusion.25 = (bf16[1,1,3,384,384]{4,3,2,1,0:T(8,128)(2,1)}, bf16[1,1,3,384,384]{4,3,2,1,0:T(8,128)(2,1)}, bf16[1,1,3,384,384]{4,3,2,1,0:T(8,128)(2,1)}, bf16[1,1...) fusion(bf16[3,3,3,384,384]{4,3,2,1,0:T(8,128)(2,1)} %param.12), kind=kLoop, calls=%fused_computation.94 | loop fusion | bytes 15925248 | tf_op jit(solution)/shard_map/slice | solution.py:74
  13.4 1.3 collective-permute-start.2
  14.7 5.5 %collective-permute-start.1 = (bf16[8,2,128,16]{2,3,1,0:T(8,128)(2,1)S(1)}, bf16[8,2,128,16]{2,3,1,0:T(8,128)(2,1)S(1)}, u32[]{:S(2)}, u32[]{:S(2)}) collective-permute-start(bf16[8,2,128,16]{2,3,1,0:T(8,128)(2,1)S(1)} %pad_maximum_fusion.11), channel_id=1, source_target_pairs={{0,2},{2,4},{4,6},{6,8},{8,10},{10,12},{12,14},{1,3},{3,5},{5,7},{... | collective-permute-start | bytes 196616 | tf_op jit(solution)/shard_map/ppermute | solution.py:25
  20.3 0.2 collective-permute-done.2
  20.6 1.6 %collective-permute-done.1 = bf16[8,2,128,16]{2,3,1,0:T(8,128)(2,1)S(1)} collective-permute-done((bf16[8,2,128,16]{2,3,1,0:T(8,128)(2,1)S(1)}, bf16[8,2,128,16]{2,3,1,0:T(8,128)(2,1)S(1)}, u32[]{:S(2)}, u32[]{:S(2)}) %collective-permute-start.1) | collective-permute-done | bytes 65568 | tf_op jit(solution)/shard_map/ppermute | solution.py:25
  24.5 1.0 copy.18
  25.6 3.2 %reshape.112 = bf16[3072,432]{0,1:T(8,128)(2,1)} reshape(bf16[6,4,128,432]{2,1,0,3:T(4,128)(2,1)S(1)} %copy.18) | data formatting | bytes 5308416 | tf_op jit(solution)/shard_map/reshape | solution.py:49
  28.7 3.6 %add_convert_fusion = bf16[3072,384]{1,0:T(8,128)(2,1)S(1)} fusion(bf16[3072,432]{0,1:T(8,128)(2,1)} %reshape.112, bf16[432,384]{1,0:T(8,128)(2,1)S(1)} %bitcast.49, f32[384]{0:T(512)S(1)} %copy-done.14), kind=kOutput, calls=%fused_computation.1 | convolution fusion | flops 1021575168 | bytes 5346816 | tf_op jit(solution)/shard_map/dot_general | solution.py:50
  32.4 0.2 convert_reduce_fusion
  32.8 32.9 %psum.14 = f32[32]{0:T(128)S(1)} all-reduce(f32[32]{0:T(128)S(1)} %reduce_sum.25), channel_id=1, replica_groups=mesh['clip'=2,'ha'=8,'ta'=2] {'ha','ta'}, use_global_device_ids=true, to_apply=%region_2.3 | all-reduce | flops 32 | bytes 256 | tf_op jit(solution)/shard_map/psum | solution.py:109
  66.0 0.3 fusion.2
  66.5 29.7 %psum.15 = f32[32]{0:T(128)S(1)} all-reduce(f32[32]{0:T(128)S(1)} %reduce_sum.37), channel_id=1, replica_groups=mesh['clip'=2,'ha'=8,'ta'=2] {'ha','ta'}, use_global_device_ids=true, to_apply=%region_5.6 | all-reduce | flops 32 | bytes 256 | tf_op jit(solution)/shard_map/psum | solution.py:111
  96.4 1.9 %fusion = bf16[6,4,128,384]{3,2,1,0:T(8,128)(2,1)S(1)} fusion(bf16[6,4,128,384]{3,2,1,0:T(8,128)(2,1)S(1)} %bitcast.53, f32[384]{0:T(512)S(1)} %copy-done.11, f32[384]{0:T(512)S(1)} %copy-done.12, f32[384]{0:T(512)S(1)} %mul.34, f32[384]{0:T(512)S(1)} %sub.26, pred[6,4]{1,0:T(8,128)(4,1)S(1)} %and_and_fusion), kind=kLoop, calls=%fused_computation.5 | loop fusion | flops 12976128 | bytes 4724760 | tf_op jit(solution)/shard_map/jit(_where)/select_n | solution.py:120
  98.3 3.6 %pad_slice_fusion.18 = (bf16[4,2,128,384]{3,2,1,0:T(8,128)(2,1)S(1)}, bf16[4,2,128,384]{3,2,1,0:T(8,128)(2,1)S(1)}, bf16[4,2,128,384]{3,2,1,0:T(8,128)(2,1)S(1)}...) fusion(bf16[6,4,128,384]{3,2,1,0:T(8,128)(2,1)S(1)} %fusion), kind=kLoop, calls=%fused_computation.76 | loop fusion | bytes 13369344 | tf_op jit(solution)/shard_map/slice | solution.py:63
  101.9 0.7 fusion.26
  102.6 3.8 %pad_slice_fusion.19 = (bf16[4,2,128,384]{3,2,1,0:T(8,128)(2,1)S(1)}, bf16[4,2,128,384]{3,2,1,0:T(8,128)(2,1)S(1)}, bf16[4,2,128,384]{3,2,1,0:T(8,128)(2,1)S(1)}...) fusion(bf16[6,4,128,384]{3,2,1,0:T(8,128)(2,1)S(1)} %fusion), kind=kLoop, calls=%fused_computation.77 | loop fusion | bytes 11010048 | tf_op jit(solution)/shard_map/slice | solution.py:63
  106.4 0.3 pad_maximum_fusion.7
  106.7 0.9 copy-done.10
  107.6 1.4 %fusion.34 = f32[1024,384]{1,0:T(8,128)S(1)} fusion(bf16[1024,1152]{1,0:T(8,128)(2,1)S(1)} %bitcast.55, bf16[1152,384]{1,0:T(8,128)(2,1)S(1)} %bitcast.72), kind=kOutput, calls=%fused_computation.103 | convolution fusion | flops 905969664 | bytes 4816896 | tf_op jit(solution)/shard_map/dot_general | solution.py:72
  109.0 0.3 pad_maximum_fusion.6
  109.3 0.9 copy-done.9
  110.2 1.4 %fusion.33 = f32[1024,384]{1,0:T(8,128)S(1)} fusion(bf16[1024,1152]{1,0:T(8,128)(2,1)S(1)} %bitcast.56, bf16[1152,384]{1,0:T(8,128)(2,1)S(1)} %bitcast.71), kind=kOutput, calls=%fused_computation.102 | convolution fusion | flops 905969664 | bytes 4816896 | tf_op jit(solution)/shard_map/dot_general | solution.py:72
  111.6 0.3 pad_maximum_fusion.5
  111.9 0.9 copy-done.8
  112.8 1.4 %fusion.32 = f32[1024,384]{1,0:T(8,128)S(1)} fusion(bf16[1024,1152]{1,0:T(8,128)(2,1)S(1)} %bitcast.57, bf16[1152,384]{1,0:T(8,128)(2,1)S(1)} %bitcast.70), kind=kOutput, calls=%fused_computation.101 | convolution fusion | flops 905969664 | bytes 4816896 | tf_op jit(solution)/shard_map/dot_general | solution.py:72
  114.2 0.3 pad_maximum_fusion.4
  114.5 0.9 copy-done.7
  115.4 1.4 %fusion.31 = f32[1024,384]{1,0:T(8,128)S(1)} fusion(bf16[1024,1152]{1,0:T(8,128)(2,1)S(1)} %bitcast.58, bf16[1152,384]{1,0:T(8,128)(2,1)S(1)} %bitcast.69), kind=kOutput, calls=%fused_computation.100 | convolution fusion | flops 905969664 | bytes 4816896 | tf_op jit(solution)/shard_map/dot_general | solution.py:72
  116.9 0.3 pad_maximum_fusion.3
  117.2 0.9 copy-done.6
  118.0 1.4 %fusion.30 = f32[1024,384]{1,0:T(8,128)S(1)} fusion(bf16[1024,1152]{1,0:T(8,128)(2,1)S(1)} %bitcast.59, bf16[1152,384]{1,0:T(8,128)(2,1)S(1)} %bitcast.68), kind=kOutput, calls=%fused_computation.99 | convolution fusion | flops 905969664 | bytes 4816896 | tf_op jit(solution)/shard_map/dot_general | solution.py:72
  119.5 0.3 pad_maximum_fusion.2
  119.8 0.9 copy-done.5
  120.6 1.4 %fusion.29 = f32[1024,384]{1,0:T(8,128)S(1)} fusion(bf16[1024,1152]{1,0:T(8,128)(2,1)S(1)} %bitcast.60, bf16[1152,384]{1,0:T(8,128)(2,1)S(1)} %bitcast.67), kind=kOutput, calls=%fused_computation.98 | convolution fusion | flops 905969664 | bytes 4816896 | tf_op jit(solution)/shard_map/dot_general | solution.py:72
  122.1 0.3 pad_maximum_fusion
  122.4 0.9 copy-done.4
  123.2 1.4 %fusion.27 = f32[1024,384]{1,0:T(8,128)S(1)} fusion(bf16[1024,1152]{1,0:T(8,128)(2,1)S(1)} %bitcast.61, bf16[1152,384]{1,0:T(8,128)(2,1)S(1)} %bitcast.66), kind=kOutput, calls=%fused_computation.96 | convolution fusion | flops 905969664 | bytes 4816896 | tf_op jit(solution)/shard_map/dot_general | solution.py:72
  124.7 0.3 pad_maximum_fusion.1
  125.0 0.9 copy-done.3
  125.8 1.4 %fusion.28 = f32[1024,384]{1,0:T(8,128)S(1)} fusion(bf16[1024,1152]{1,0:T(8,128)(2,1)S(1)} %bitcast.62, bf16[1152,384]{1,0:T(8,128)(2,1)S(1)} %bitcast.65), kind=kOutput, calls=%fused_computation.97 | convolution fusion | flops 905969664 | bytes 4816896 | tf_op jit(solution)/shard_map/dot_general | solution.py:72
  127.3 0.3 pad_maximum_fusion.8
  127.6 0.9 copy-done.2
  128.5 1.7 %add_add_fusion = f32[1024,384]{1,0:T(8,128)S(1)} fusion(f32[1024,384]{1,0:T(8,128)S(1)} %fusion.34, f32[1024,384]{1,0:T(8,128)S(1)} %fusion.33, f32[1024,384]{1,0:T(8,128)S(1)} %fusion.32, f32[1024,384]{1,0:T(8,128)S(1)} %fusion.31, f32[1024,384]{1,0:T(8,128)S(1)} %fusion.30, f32[1024,384]{1,0:T(8,128)S(1)} %fusion.29, f32[1024,384]{1,0:T(8,128)S(1)} %fusion.27, ...), kind=kOutput, calls=%fused_computation.19 | convolution fusion | flops 909115392 | bytes 17399808 | tf_op jit(solution)/shard_map/dot_general | solution.py:72
  130.2 1.1 fusion.4
  (71 shorter events, 3.8 us)
Async XLA Ops:
  0.0 28.7 %copy-start = (bf16[3,3,3,16,384]{4,3,2,1,0:T(8,128)(2,1)S(1)}, bf16[3,3,3,16,384]{4,3,2,1,0:T(8,128)(2,1)}, u32[]{:S(2)}) copy-start(bf16[3,3,3,16,384]{4,3,2,1,0:T(8,128)(2,1)} %param.8) | copy-start | bytes 995332
  5.3 8.0 %collective-permute-start = (bf16[4,2,128,16]{3,2,1,0:T(8,128)(2,1)S(1)}, bf16[4,2,128,16]{3,2,1,0:T(8,128)(2,1)S(1)}, u32[]{:S(2)}, u32[]{:S(2)}) collective-permute-start(bf16[4,2,128,16]{3,2,1,0:T(8,128)(2,1)S(1)} %bitcast.63), channel_id=1, source_target_pairs={{0,1},{2,3},{4,5},{6,7},{8,9},{10,11},{12,13},{14,15},{16,17},{18,... | collective-permute-start | bytes 98312 | tf_op jit(solution)/shard_map/ppermute | solution.py:15
  13.4 7.1 %collective-permute-start.2 = (bf16[8,2,128,16]{2,3,1,0:T(8,128)(2,1)S(1)}, bf16[8,2,128,16]{2,3,1,0:T(8,128)(2,1)S(1)}, u32[]{:S(2)}, u32[]{:S(2)}) collective-permute-start(bf16[8,2,128,16]{2,3,1,0:T(8,128)(2,1)S(1)} %pad_maximum_fusion.11), channel_id=1, source_target_pairs={{2,0},{4,2},{6,4},{8,6},{10,8},{12,10},{14,12},{3,1},{5,3},{7,5},{... | collective-permute-start | bytes 196616 | tf_op jit(solution)/shard_map/ppermute | solution.py:26
  14.7 7.4 %collective-permute-start.1 = (bf16[8,2,128,16]{2,3,1,0:T(8,128)(2,1)S(1)}, bf16[8,2,128,16]{2,3,1,0:T(8,128)(2,1)S(1)}, u32[]{:S(2)}, u32[]{:S(2)}) collective-permute-start(bf16[8,2,128,16]{2,3,1,0:T(8,128)(2,1)S(1)} %pad_maximum_fusion.11), channel_id=1, source_target_pairs={{0,2},{2,4},{4,6},{6,8},{8,10},{10,12},{12,14},{1,3},{3,5},{5,7},{... | collective-permute-start | bytes 196616 | tf_op jit(solution)/shard_map/ppermute | solution.py:25
  25.5 3.2 %copy-start.14 = (f32[384]{0:T(512)S(1)}, f32[384]{0:T(512)}, u32[]{:S(2)}) copy-start(f32[384]{0:T(512)} %param.9) | copy-start | bytes 4612
  32.3 64.0 %copy-start.11 = (f32[384]{0:T(512)S(1)}, f32[384]{0:T(512)}, u32[]{:S(2)}) copy-start(f32[384]{0:T(512)} %param.11) | copy-start | bytes 4612
  32.3 64.0 %copy-start.12 = (f32[384]{0:T(512)S(1)}, f32[384]{0:T(512)}, u32[]{:S(2)}) copy-start(f32[384]{0:T(512)} %param.10) | copy-start | bytes 4612
  106.4 1.2 copy-start.10
  109.0 1.2 copy-start.9
  111.6 1.2 copy-start.8
  114.2 1.2 copy-start.7
  116.8 1.2 copy-start.6
  119.5 1.2 copy-start.5
  122.1 1.2 copy-start.4
  124.7 1.2 copy-start.3
  127.3 1.2 copy-start.2
  128.5 1.8 %copy-start.13 = (f32[384]{0:T(512)S(1)}, f32[384]{0:T(512)}, u32[]{:S(2)}) copy-start(f32[384]{0:T(512)} %param.13) | copy-start | bytes 4612
  128.5 2.9 %copy-start.1 = (bf16[3,3,3,16,384]{4,3,2,1,0:T(8,128)(2,1)S(1)}, bf16[3,3,3,16,384]{4,3,2,1,0:T(8,128)(2,1)}, u32[]{:S(2)}) copy-start(bf16[3,3,3,16,384]{4,3,2,1,0:T(8,128)(2,1)} %param.8) | copy-start | bytes 995332
where the time goes:
time: 132 us; the launch traced here: 131 us
  blocking collectives  66.4 us (50%)
  local copies, waits for them, and re-layouts  30.3 us (23%)
  matrix products  16.8 us (13%)
  starting transfers between devices  8.88 us (7%)
  other arithmetic  6.55 us (5%)
  waiting for transfers between devices  1.81 us (1%)
    psum x1, blocking collectives, body(): mean = lax.psum(group_totals(values), ('ha', 'ta')) / count  32.9 us
    psum x1, blocking collectives, body(): var = lax.psum(group_totals(centered * centered), ('ha', 'ta')) / count  29.7 us
    dot_general x9, matrix products, middle_conv(): jnp.dot(slab, w_mid[frame_tap, row_tap].reshape(3 * channels, -1), prefer...  13.2 us
    unnamed x58, local copies, waits for them, and re-layouts  10.8 us
    slice x3, local copies, waits for them, and re-layouts, middle_conv(): padded[frame_tap:frame_tap + frames, row_tap:row_tap + rows, col_tap:col_...  8.12 us
    slice x1, local copies, waits for them, and re-layouts, middle_conv(): w_mid[frame_tap, row_tap].reshape(3 * channels, -1)  5.75 us
    ppermute x1, starting transfers between devices, extended_2(): before = lax.ppermute(last, axis, up)  5.5 us
    all_to_all x1, blocking collectives, body(): lax.all_to_all(latent_tokens, 'ta', split_axis=0, concat_axis=1, tiled=True)  3.75 us
  transfers between devices with their start and end apart: 3, of which 2 were waited for; matrix products, arithmetic and copies ran while one was open for 5% of the time, Pallas kernels for 0%

commit v1 on v0

--- a/solution.py
+++ b/solution.py
@@ -106,7 +106,7 @@
     values = lax.optimization_barrier(hidden).astype(jnp.float32)
     members = values.shape[-1] // GROUPS
     count = float(lax.axis_size("ha") * lax.axis_size("ta") * frames * rows * cols * members)
-    mean = lax.psum(group_totals(values), ("ha", "ta")) / count
+    mean = jnp.sum(lax.all_gather(group_totals(values), ("ha", "ta")), axis=0) / count
     centered = values - jnp.repeat(mean, members)
     var = lax.psum(group_totals(centered * centered), ("ha", "ta")) / count
     active = normalize(wide_hidden, mean, var, gn_gain, gn_shift)

time: 132 us -> 132 us (level)
    psum x1 -> x0, blocking collectives: 32.9 us -> none  [body(): mean = lax.psum(group_totals(values), ('ha', 'ta')) / count]
    unnamed x0 -> x1, blocking collectives: none -> 32.9 us
    unnamed x58 -> x63, local copies, waits for them, and re-layouts: 10.8 us -> 11.7 us
  transfers between devices with their start and end apart: 3 -> 3, of which waited for: 2 -> 1; matrix products, arithmetic and copies ran while one was open for 5% -> 5% of each run, Pallas kernels for 0% -> 0%
where the time goes in v1:
time: 132 us
  blocking collectives  66.3 us (50%)
  local copies, waits for them, and re-layouts  31.2 us (24%)
  matrix products  16.8 us (13%)
  starting transfers between devices  8.88 us (7%)
  other arithmetic  6.57 us (5%)
  between operations  1.32 us (1%)
    unnamed x1, blocking collectives  32.9 us
    psum x1, blocking collectives, body(): var = lax.psum(group_totals(centered * centered), ('ha', 'ta')) / count  29.7 us
    dot_general x9, matrix products, middle_conv(): jnp.dot(slab, w_mid[frame_tap, row_tap].reshape(3 * channels, -1), prefer...  13.2 us
    unnamed x63, local copies, waits for them, and re-layouts  11.7 us
    slice x3, local copies, waits for them, and re-layouts, middle_conv(): padded[frame_tap:frame_tap + frames, row_tap:row_tap + rows, col_tap:col_...  8.12 us
    slice x1, local copies, waits for them, and re-layouts, middle_conv(): w_mid[frame_tap, row_tap].reshape(3 * channels, -1)  5.75 us
    ppermute x1, starting transfers between devices, extended_2(): before = lax.ppermute(last, axis, up)  5.5 us
    all_to_all x1, blocking collectives, body(): lax.all_to_all(latent_tokens, 'ta', split_axis=0, concat_axis=1, tiled=True)  3.75 us
  transfers between devices with their start and end apart: 3, of which 1 were waited for; matrix products, arithmetic and copies ran while one was open for 5% of the time, Pallas kernels for 0%

profile of v1, /device:TPU:0, one launch (start us, length us, event | category | flops | bytes accessed | tf_op | source)
XLA Modules:
  0.0 131.7 jit_solution(9019811404995285617)
XLA Ops:
  0.0 1.0 reshape.130
  1.0 3.7 %all_to_all.15 = bf16[2,2,4096]{2,1,0:T(2,128)(2,1)S(1)} all-to-all(bf16[2,2,4096]{2,1,0:T(2,128)(2,1)S(1)} %reshape.130), channel_id=1, replica_groups=mesh['clip'=2,'ha'=8,'ta'=2] {'ta'}, dimensions={0} | all-to-all | bytes 65536 | tf_op jit(solution)/shard_map/all_to_all | solution.py:96
  5.3 2.1 %collective-permute-start = (bf16[4,2,128,16]{3,2,1,0:T(8,128)(2,1)S(1)}, bf16[4,2,128,16]{3,2,1,0:T(8,128)(2,1)S(1)}, u32[]{:S(2)}, u32[]{:S(2)}) collective-permute-start(bf16[4,2,128,16]{3,2,1,0:T(8,128)(2,1)S(1)} %bitcast.64), channel_id=1, source_target_pairs={{0,1},{2,3},{4,5},{6,7},{8,9},{10,11},{12,13},{14,15},{16,17},{18,... | collective-permute-start | bytes 98312 | tf_op jit(solution)/shard_map/ppermute | solution.py:15
  7.4 5.7 %fusion.25 = (bf16[1,1,3,384,384]{4,3,2,1,0:T(8,128)(2,1)}, bf16[1,1,3,384,384]{4,3,2,1,0:T(8,128)(2,1)}, bf16[1,1,3,384,384]{4,3,2,1,0:T(8,128)(2,1)}, bf16[1,1...) fusion(bf16[3,3,3,384,384]{4,3,2,1,0:T(8,128)(2,1)} %param.12), kind=kLoop, calls=%fused_computation.94 | loop fusion | bytes 15925248 | tf_op jit(solution)/shard_map/slice | solution.py:74
  13.5 1.3 collective-permute-start.2
  14.8 5.5 %collective-permute-start.1 = (bf16[8,2,128,16]{2,3,1,0:T(8,128)(2,1)S(1)}, bf16[8,2,128,16]{2,3,1,0:T(8,128)(2,1)S(1)}, u32[]{:S(2)}, u32[]{:S(2)}) collective-permute-start(bf16[8,2,128,16]{2,3,1,0:T(8,128)(2,1)S(1)} %pad_maximum_fusion.11), channel_id=1, source_target_pairs={{0,2},{2,4},{4,6},{6,8},{8,10},{10,12},{12,14},{1,3},{3,5},{5,7},{... | collective-permute-start | bytes 196616 | tf_op jit(solution)/shard_map/ppermute | solution.py:25
  20.3 0.6 dynamic-slice
  21.6 0.6 collective-permute-done.1
  24.5 1.0 copy.23
  25.6 3.2 %reshape.112 = bf16[3072,432]{0,1:T(8,128)(2,1)} reshape(bf16[6,4,128,432]{2,1,0,3:T(4,128)(2,1)S(1)} %copy.23) | data formatting | bytes 5308416 | tf_op jit(solution)/shard_map/reshape | solution.py:49
  28.7 3.6 %add_convert_fusion = bf16[3072,384]{1,0:T(8,128)(2,1)S(1)} fusion(bf16[3072,432]{0,1:T(8,128)(2,1)} %reshape.112, bf16[432,384]{1,0:T(8,128)(2,1)S(1)} %bitcast.50, f32[384]{0:T(512)S(1)} %copy-done.14), kind=kOutput, calls=%fused_computation.1 | convolution fusion | flops 1021575168 | bytes 5346816 | tf_op jit(solution)/shard_map/dot_general | solution.py:50
  32.5 0.2 convert_reduce_fusion
  32.9 0.2 dynamic-update-slice
  33.1 32.9 %all-reduce.2 = f32[512]{0:T(512)S(1)} all-reduce(f32[512]{0:T(512)S(1)} %dynamic-update-slice), channel_id=2, replica_groups=mesh['clip'=2,'ha'=8,'ta'=2] {'ha','ta'}, use_global_device_ids=true, to_apply=%add.2 | all-reduce | flops 512 | bytes 4096
  66.3 0.3 fusion.2
  66.8 29.7 %psum.7 = f32[32]{0:T(128)S(1)} all-reduce(f32[32]{0:T(128)S(1)} %reduce_sum.47), channel_id=1, replica_groups=mesh['clip'=2,'ha'=8,'ta'=2] {'ha','ta'}, use_global_device_ids=true, to_apply=%region_5.6 | all-reduce | flops 32 | bytes 256 | tf_op jit(solution)/shard_map/psum | solution.py:111
  96.7 1.9 %fusion = bf16[6,4,128,384]{3,2,1,0:T(8,128)(2,1)S(1)} fusion(bf16[6,4,128,384]{3,2,1,0:T(8,128)(2,1)S(1)} %bitcast.54, f32[384]{0:T(512)S(1)} %copy-done.11, f32[384]{0:T(512)S(1)} %copy-done.12, f32[384]{0:T(512)S(1)} %mul.34, f32[384]{0:T(512)S(1)} %sub.26, pred[6,4]{1,0:T(8,128)(4,1)S(1)} %and_and_fusion), kind=kLoop, calls=%fused_computation.5 | loop fusion | flops 12976128 | bytes 4724760 | tf_op jit(solution)/shard_map/jit(_where)/select_n | solution.py:120
  98.6 3.6 %pad_slice_fusion.18 = (bf16[4,2,128,384]{3,2,1,0:T(8,128)(2,1)S(1)}, bf16[4,2,128,384]{3,2,1,0:T(8,128)(2,1)S(1)}, bf16[4,2,128,384]{3,2,1,0:T(8,128)(2,1)S(1)}...) fusion(bf16[6,4,128,384]{3,2,1,0:T(8,128)(2,1)S(1)} %fusion), kind=kLoop, calls=%fused_computation.76 | loop fusion | bytes 13369344 | tf_op jit(solution)/shard_map/slice | solution.py:63
  102.2 0.7 fusion.26
  102.9 3.8 %pad_slice_fusion.19 = (bf16[4,2,128,384]{3,2,1,0:T(8,128)(2,1)S(1)}, bf16[4,2,128,384]{3,2,1,0:T(8,128)(2,1)S(1)}, bf16[4,2,128,384]{3,2,1,0:T(8,128)(2,1)S(1)}...) fusion(bf16[6,4,128,384]{3,2,1,0:T(8,128)(2,1)S(1)} %fusion), kind=kLoop, calls=%fused_computation.77 | loop fusion | bytes 11010048 | tf_op jit(solution)/shard_map/slice | solution.py:63
  106.8 0.3 pad_maximum_fusion.7
  107.1 0.9 copy-done.10
  107.9 1.4 %fusion.34 = f32[1024,384]{1,0:T(8,128)S(1)} fusion(bf16[1024,1152]{1,0:T(8,128)(2,1)S(1)} %bitcast.56, bf16[1152,384]{1,0:T(8,128)(2,1)S(1)} %bitcast.73), kind=kOutput, calls=%fused_computation.103 | convolution fusion | flops 905969664 | bytes 4816896 | tf_op jit(solution)/shard_map/dot_general | solution.py:72
  109.4 0.3 pad_maximum_fusion.6
  109.7 0.9 copy-done.9
  110.5 1.4 %fusion.33 = f32[1024,384]{1,0:T(8,128)S(1)} fusion(bf16[1024,1152]{1,0:T(8,128)(2,1)S(1)} %bitcast.57, bf16[1152,384]{1,0:T(8,128)(2,1)S(1)} %bitcast.72), kind=kOutput, calls=%fused_computation.102 | convolution fusion | flops 905969664 | bytes 4816896 | tf_op jit(solution)/shard_map/dot_general | solution.py:72
  112.0 0.3 pad_maximum_fusion.5
  112.3 0.9 copy-done.8
  113.1 1.4 %fusion.32 = f32[1024,384]{1,0:T(8,128)S(1)} fusion(bf16[1024,1152]{1,0:T(8,128)(2,1)S(1)} %bitcast.58, bf16[1152,384]{1,0:T(8,128)(2,1)S(1)} %bitcast.71), kind=kOutput, calls=%fused_computation.101 | convolution fusion | flops 905969664 | bytes 4816896 | tf_op jit(solution)/shard_map/dot_general | solution.py:72
  114.6 0.3 pad_maximum_fusion.4
  114.9 0.9 copy-done.7
  115.8 1.4 %fusion.31 = f32[1024,384]{1,0:T(8,128)S(1)} fusion(bf16[1024,1152]{1,0:T(8,128)(2,1)S(1)} %bitcast.59, bf16[1152,384]{1,0:T(8,128)(2,1)S(1)} %bitcast.70), kind=kOutput, calls=%fused_computation.100 | convolution fusion | flops 905969664 | bytes 4816896 | tf_op jit(solution)/shard_map/dot_general | solution.py:72
  117.2 0.3 pad_maximum_fusion.3
  117.5 0.9 copy-done.6
  118.4 1.4 %fusion.30 = f32[1024,384]{1,0:T(8,128)S(1)} fusion(bf16[1024,1152]{1,0:T(8,128)(2,1)S(1)} %bitcast.60, bf16[1152,384]{1,0:T(8,128)(2,1)S(1)} %bitcast.69), kind=kOutput, calls=%fused_computation.99 | convolution fusion | flops 905969664 | bytes 4816896 | tf_op jit(solution)/shard_map/dot_general | solution.py:72
  119.8 0.3 pad_maximum_fusion.2
  120.1 0.9 copy-done.5
  121.0 1.4 %fusion.29 = f32[1024,384]{1,0:T(8,128)S(1)} fusion(bf16[1024,1152]{1,0:T(8,128)(2,1)S(1)} %bitcast.61, bf16[1152,384]{1,0:T(8,128)(2,1)S(1)} %bitcast.68), kind=kOutput, calls=%fused_computation.98 | convolution fusion | flops 905969664 | bytes 4816896 | tf_op jit(solution)/shard_map/dot_general | solution.py:72
  122.4 0.3 pad_maximum_fusion
  122.7 0.9 copy-done.4
  123.6 1.4 %fusion.27 = f32[1024,384]{1,0:T(8,128)S(1)} fusion(bf16[1024,1152]{1,0:T(8,128)(2,1)S(1)} %bitcast.62, bf16[1152,384]{1,0:T(8,128)(2,1)S(1)} %bitcast.67), kind=kOutput, calls=%fused_computation.96 | convolution fusion | flops 905969664 | bytes 4816896 | tf_op jit(solution)/shard_map/dot_general | solution.py:72
  125.0 0.3 pad_maximum_fusion.1
  125.3 0.9 copy-done.3
  126.2 1.4 %fusion.28 = f32[1024,384]{1,0:T(8,128)S(1)} fusion(bf16[1024,1152]{1,0:T(8,128)(2,1)S(1)} %bitcast.63, bf16[1152,384]{1,0:T(8,128)(2,1)S(1)} %bitcast.66), kind=kOutput, calls=%fused_computation.97 | convolution fusion | flops 905969664 | bytes 4816896 | tf_op jit(solution)/shard_map/dot_general | solution.py:72
  127.6 0.3 pad_maximum_fusion.8
  127.9 0.9 copy-done.2
  128.8 1.7 %add_add_fusion = f32[1024,384]{1,0:T(8,128)S(1)} fusion(f32[1024,384]{1,0:T(8,128)S(1)} %fusion.34, f32[1024,384]{1,0:T(8,128)S(1)} %fusion.33, f32[1024,384]{1,0:T(8,128)S(1)} %fusion.32, f32[1024,384]{1,0:T(8,128)S(1)} %fusion.31, f32[1024,384]{1,0:T(8,128)S(1)} %fusion.30, f32[1024,384]{1,0:T(8,128)S(1)} %fusion.29, f32[1024,384]{1,0:T(8,128)S(1)} %fusion.27, ...), kind=kOutput, calls=%fused_computation.19 | convolution fusion | flops 909115392 | bytes 17399808 | tf_op jit(solution)/shard_map/dot_general | solution.py:72
  130.6 1.1 fusion.4
  (78 shorter events, 4.1 us)
Async XLA Ops:
  0.0 28.7 %copy-start = (bf16[3,3,3,16,384]{4,3,2,1,0:T(8,128)(2,1)S(1)}, bf16[3,3,3,16,384]{4,3,2,1,0:T(8,128)(2,1)}, u32[]{:S(2)}) copy-start(bf16[3,3,3,16,384]{4,3,2,1,0:T(8,128)(2,1)} %param.8) | copy-start | bytes 995332
  5.3 8.0 %collective-permute-start = (bf16[4,2,128,16]{3,2,1,0:T(8,128)(2,1)S(1)}, bf16[4,2,128,16]{3,2,1,0:T(8,128)(2,1)S(1)}, u32[]{:S(2)}, u32[]{:S(2)}) collective-permute-start(bf16[4,2,128,16]{3,2,1,0:T(8,128)(2,1)S(1)} %bitcast.64), channel_id=1, source_target_pairs={{0,1},{2,3},{4,5},{6,7},{8,9},{10,11},{12,13},{14,15},{16,17},{18,... | collective-permute-start | bytes 98312 | tf_op jit(solution)/shard_map/ppermute | solution.py:15
  7.4 12.9 %copy-start.15 = (u32[32]{0:T(128)S(1)}, u32[32]{0:T(128)}, u32[]{:S(2)}) copy-start(u32[32]{0:T(128)} %constant.44) | copy-start | bytes 388
  13.5 8.1 %collective-permute-start.2 = (bf16[8,2,128,16]{2,3,1,0:T(8,128)(2,1)S(1)}, bf16[8,2,128,16]{2,3,1,0:T(8,128)(2,1)S(1)}, u32[]{:S(2)}, u32[]{:S(2)}) collective-permute-start(bf16[8,2,128,16]{2,3,1,0:T(8,128)(2,1)S(1)} %pad_maximum_fusion.11), channel_id=1, source_target_pairs={{2,0},{4,2},{6,4},{8,6},{10,8},{12,10},{14,12},{3,1},{5,3},{7,5},{... | collective-permute-start | bytes 196616 | tf_op jit(solution)/shard_map/ppermute | solution.py:26
  14.8 7.4 %collective-permute-start.1 = (bf16[8,2,128,16]{2,3,1,0:T(8,128)(2,1)S(1)}, bf16[8,2,128,16]{2,3,1,0:T(8,128)(2,1)S(1)}, u32[]{:S(2)}, u32[]{:S(2)}) collective-permute-start(bf16[8,2,128,16]{2,3,1,0:T(8,128)(2,1)S(1)} %pad_maximum_fusion.11), channel_id=1, source_target_pairs={{0,2},{2,4},{4,6},{6,8},{8,10},{10,12},{12,14},{1,3},{3,5},{5,7},{... | collective-permute-start | bytes 196616 | tf_op jit(solution)/shard_map/ppermute | solution.py:25
  25.6 3.2 %copy-start.14 = (f32[384]{0:T(512)S(1)}, f32[384]{0:T(512)}, u32[]{:S(2)}) copy-start(f32[384]{0:T(512)} %param.9) | copy-start | bytes 4612
  32.3 64.4 %copy-start.11 = (f32[384]{0:T(512)S(1)}, f32[384]{0:T(512)}, u32[]{:S(2)}) copy-start(f32[384]{0:T(512)} %param.11) | copy-start | bytes 4612
  32.3 64.4 %copy-start.12 = (f32[384]{0:T(512)S(1)}, f32[384]{0:T(512)}, u32[]{:S(2)}) copy-start(f32[384]{0:T(512)} %param.10) | copy-start | bytes 4612
  106.8 1.2 copy-start.10
  109.4 1.2 copy-start.9
  112.0 1.2 copy-start.8
  114.6 1.2 copy-start.7
  117.2 1.2 copy-start.6
  119.8 1.2 copy-start.5
  122.4 1.2 copy-start.4
  125.0 1.2 copy-start.3
  127.6 1.2 copy-start.2
  128.8 1.8 %copy-start.13 = (f32[384]{0:T(512)S(1)}, f32[384]{0:T(512)}, u32[]{:S(2)}) copy-start(f32[384]{0:T(512)} %param.13) | copy-start | bytes 4612
  128.8 2.9 %copy-start.1 = (bf16[3,3,3,16,384]{4,3,2,1,0:T(8,128)(2,1)S(1)}, bf16[3,3,3,16,384]{4,3,2,1,0:T(8,128)(2,1)}, u32[]{:S(2)}) copy-start(bf16[3,3,3,16,384]{4,3,2,1,0:T(8,128)(2,1)} %param.8) | copy-start | bytes 995332
